TPU v7x, 32 devices: a whole 2x2x4 slice. The times are simulated.
32 devices in a mesh: body: 2 (over y), gx: 4 (over z), gy: 2 (over x), gz: 2 (over core).
Axes of the slice: x: 2, y: 2, z: 4, core: 2. Of those that a mesh axis runs over, the one named last changes fastest.
Arguments:
- fields: float32 [4, 3, 16, 16, 256], P('body', None, 'gx', 'gy', 'gz'), parts along dimension 0, may hold values from -0.06 to 0.06
- macro_strain: float32 [6, 3], P('body'), parts along dimension 0, may hold values from -0.15 to 0.15
- material: float32 [4], P('body'), parts along dimension 0, may hold values from 2 to 10
Outputs:
- residual: float32 [6, 16, 16, 256], P('body', 'gx', 'gy', 'gz'), parts along dimension 0
- tangent: float32 [6, 16, 16, 256], P('body', 'gx', 'gy', 'gz'), parts along dimension 0
- stats: float32 [4], P('body'), parts along dimension 0
There are 2 independent parts, one for each index of `body`. A program takes and returns all parts, laid end to end along the dimension named above; each array names one. Nothing has to cross between parts.
All inputs are finite; a program needn't handle non-finite values.
Results may differ from a plain program's by a relative error of at most 0.0002.
Values sent between devices are 32-bit elements; how exact they have to be, the bound alone decides.
A program may use at most 64 MiB of HBM per device.

v0:
```python
import math

import jax
import jax.numpy as jnp
import numpy as np
from jax import lax
from jax.sharding import PartitionSpec as P

highest = lax.Precision.HIGHEST
spacing = 4.0
root_eps = 1e-06


def passed_along(block, axis, distance):
    devices = range(lax.axis_size(axis))
    route = [((i - distance) % len(devices), i) for i in devices]
    return lax.ppermute(block, axis, route)


def shape_tables():
    gauss_root = math.sqrt(0.6)
    points = np.array([-gauss_root, 0.0, gauss_root])
    values = np.stack(
        [points * (points - 1.0) / 2.0, 1.0 - points * points, points * (points + 1.0) / 2.0],
        axis=1,
    )
    slopes = np.stack([points - 0.5, -2.0 * points, points + 0.5], axis=1) * (2.0 / spacing)
    weights = np.array([5.0 / 9.0, 8.0 / 9.0, 5.0 / 9.0])
    volume = (
        weights[:, None, None]
        * weights[None, :, None]
        * weights[None, None, :]
        * (spacing / 2.0) ** 3
    )
    return (
        jnp.asarray(values, jnp.float32),
        jnp.asarray(slopes, jnp.float32),
        jnp.asarray(volume, jnp.float32),
    )


def triplets(array, axis):
    elements = (array.shape[axis] - 1) // 2
    even_nodes = lax.slice_in_dim(array, 0, 2 * elements, 2, axis)
    odd_nodes = lax.slice_in_dim(array, 1, 2 * elements, 2, axis)
    next_nodes = lax.slice_in_dim(array, 2, 2 * elements + 1, 2, axis)
    return jnp.stack([even_nodes, odd_nodes, next_nodes], axis=2)


def scatter_back(stacked):
    pieces = [lax.index_in_dim(stacked, slot_index, 2, keepdims=False) for slot_index in range(3)]
    pad_after = [(0, 0)] * pieces[0].ndim
    pad_after[3] = (0, 1)
    pad_before = [(0, 0)] * pieces[0].ndim
    pad_before[3] = (1, 0)
    even_nodes = jnp.pad(pieces[0], pad_after) + jnp.pad(pieces[2], pad_before)
    odd_nodes = jnp.pad(pieces[1], pad_after)
    paired = jnp.stack([even_nodes, odd_nodes], axis=4)
    merged_shape = paired.shape[:3] + (2 * paired.shape[3],) + paired.shape[5:]
    merged = paired.reshape(merged_shape)
    return lax.slice_in_dim(merged, 0, merged.shape[3] - 1, 1, 3)


def stresses(grads, strain, shear, lame_first):
    deform = [
        [
            grads[col_at][row_at] + strain[row_at, col_at] + (1.0 if row_at == col_at else 0.0)
            for col_at in range(3)
        ]
        for row_at in range(3)
    ]
    change = [[grads[col_at][3 + row_at] for col_at in range(3)] for row_at in range(3)]
    cofactor = [
        [
            deform[(row_at + 1) % 3][(col_at + 1) % 3] * deform[(row_at + 2) % 3][(col_at + 2) % 3]
            - deform[(row_at + 1) % 3][(col_at + 2) % 3]
            * deform[(row_at + 2) % 3][(col_at + 1) % 3]
            for col_at in range(3)
        ]
        for row_at in range(3)
    ]
    volume_ratio = (
        deform[0][0] * cofactor[0][0]
        + deform[0][1] * cofactor[0][1]
        + deform[0][2] * cofactor[0][2]
    )
    inverse_t = [
        [cofactor[row_at][col_at] / volume_ratio for col_at in range(3)] for row_at in range(3)
    ]
    log_ratio = jnp.log(volume_ratio)
    stress = [
        [
            shear * (deform[row_at][col_at] - inverse_t[row_at][col_at])
            + lame_first * log_ratio * inverse_t[row_at][col_at]
            for col_at in range(3)
        ]
        for row_at in range(3)
    ]
    trace_term = sum(
        (
            inverse_t[row_at][col_at] * change[row_at][col_at]
            for row_at in range(3)
            for col_at in range(3)
        )
    )
    product = [
        [
            sum((inverse_t[row_at][mid_at] * change[col_at][mid_at] for mid_at in range(3)))
            for col_at in range(3)
        ]
        for row_at in range(3)
    ]
    twisted = [
        [
            sum((product[row_at][mid_at] * inverse_t[mid_at][col_at] for mid_at in range(3)))
            for col_at in range(3)
        ]
        for row_at in range(3)
    ]
    softening = shear - lame_first * log_ratio
    dstress = [
        [
            shear * change[row_at][col_at]
            + softening * twisted[row_at][col_at]
            + lame_first * trace_term * inverse_t[row_at][col_at]
            for col_at in range(3)
        ]
        for row_at in range(3)
    ]
    return (stress, dstress)


def layer_forces(slab_nodes, strain, material):
    values, slopes, volume = shape_tables()
    grid_stack = triplets(triplets(slab_nodes, 3), 3)
    grid_shape = grid_stack.shape
    stacked = grid_stack.reshape(grid_shape[:4] + (1, grid_shape[4] * grid_shape[5]))
    z_value = jnp.einsum("qa,cxyaij->cxyqij", values, stacked, precision=highest)
    z_slope = jnp.einsum("qa,cxyaij->cxyqij", slopes, stacked, precision=highest)
    y_value = jnp.einsum("qa,cxazij->cxqzij", values, z_value, precision=highest)
    y_slope = jnp.einsum("qa,cxazij->cxqzij", slopes, z_value, precision=highest)
    yz_slope = jnp.einsum("qa,cxazij->cxqzij", values, z_slope, precision=highest)
    grads = [
        jnp.einsum("qa,cayzij->cqyzij", slopes, y_value, precision=highest),
        jnp.einsum("qa,cayzij->cqyzij", values, y_slope, precision=highest),
        jnp.einsum("qa,cayzij->cqyzij", values, yz_slope, precision=highest),
    ]
    stress, dstress = stresses(grads, strain, material[0], material[1])
    weight = volume[:, :, :, None, None]
    fluxes = [
        jnp.stack(
            [
                stress[0][along],
                stress[1][along],
                stress[2][along],
                dstress[0][along],
                dstress[1][along],
                dstress[2][along],
            ]
        )
        * weight
        for along in range(3)
    ]
    back_x0 = jnp.einsum("qa,cqyzij->cayzij", slopes, fluxes[0], precision=highest)
    back_x1 = jnp.einsum("qa,cqyzij->cayzij", values, fluxes[1], precision=highest)
    back_x2 = jnp.einsum("qa,cqyzij->cayzij", values, fluxes[2], precision=highest)
    back_y = jnp.einsum("qa,cxqzij->cxazij", values, back_x0, precision=highest) + jnp.einsum(
        "qa,cxqzij->cxazij", slopes, back_x1, precision=highest
    )
    back_yz = jnp.einsum("qa,cxqzij->cxazij", values, back_x2, precision=highest)
    back_z = jnp.einsum("qa,cxyqij->cxyaij", values, back_y, precision=highest) + jnp.einsum(
        "qa,cxyqij->cxyaij", slopes, back_yz, precision=highest
    )
    return scatter_back(scatter_back(back_z.reshape(grid_shape)))


def assemble(nodes, macro_strain, material):
    layers = (nodes.shape[1] - 1) // 2

    def one_layer(layer_index, accumulated):
        plane_start = (2 * layer_index).astype(jnp.int32)
        slab_nodes = lax.dynamic_slice_in_dim(nodes, plane_start, 3, 1)
        contribution = layer_forces(slab_nodes, macro_strain, material)
        current = lax.dynamic_slice_in_dim(accumulated, plane_start, 3, 1)
        return lax.dynamic_update_slice_in_dim(accumulated, current + contribution, plane_start, 1)

    return lax.fori_loop(0, layers, one_layer, jnp.zeros(nodes.shape, jnp.float32))


def fold_upper(accumulated, spilled, axis):
    first = lax.slice_in_dim(accumulated, 0, 1, 1, axis) + spilled
    middle = lax.slice_in_dim(accumulated, 1, accumulated.shape[axis] - 1, 1, axis)
    return jnp.concatenate([first, middle], axis=axis)


def local(fields, macro_strain, material):
    flat = fields.reshape((6,) + fields.shape[2:])
    nodes = flat
    upper = passed_along(nodes[:, :1], "gx", -1)
    nodes = jnp.concatenate([nodes, upper], axis=1)
    upper = passed_along(nodes[:, :, :1], "gy", -1)
    nodes = jnp.concatenate([nodes, upper], axis=2)
    upper = passed_along(nodes[:, :, :, :1], "gz", -1)
    nodes = jnp.concatenate([nodes, upper], axis=3)
    accumulated = assemble(nodes, macro_strain, material)
    spilled = passed_along(accumulated[:, :, :, -1:], "gz", 1)
    accumulated = fold_upper(accumulated, spilled, 3)
    spilled = passed_along(accumulated[:, :, -1:], "gy", 1)
    accumulated = fold_upper(accumulated, spilled, 2)
    spilled = passed_along(accumulated[:, -1:], "gx", 1)
    owned = fold_upper(accumulated, spilled, 1)
    residual = owned[:3]
    tangent = owned[3:]
    squares = jnp.sum(residual * residual)
    curvature = jnp.sum(flat[3:] * tangent)
    totals = lax.psum((squares, curvature), ("gx", "gy", "gz"))
    entries = (
        3.0
        * flat.shape[1]
        * flat.shape[2]
        * flat.shape[3]
        * lax.axis_size("gx")
        * lax.axis_size("gy")
        * lax.axis_size("gz")
    )
    stats = jnp.stack([jnp.sqrt(totals[0] / entries + root_eps), totals[1] / entries])
    return (residual, tangent, stats)


def solution(mesh):
    in_specs = (P("body", None, "gx", "gy", "gz"), P("body", None), P("body"))
    out_specs = (P("body", "gx", "gy", "gz"), P("body", "gx", "gy", "gz"), P("body"))
    return jax.shard_map(local, mesh=mesh, in_specs=in_specs, out_specs=out_specs, check_vma=False)
```

profile of v0, /device:TPU:0, one launch (start us, length us, event | category | flops | bytes accessed | tf_op | source)
XLA Modules:
  0.0 190.6 jit_solution(1717546106372409096)
XLA Ops:
  1.6 5.1 %collective-permute-start = (f32[6,1,8,128]{3,2,0,1:T(8,128)S(1)}, f32[6,1,8,128]{3,2,0,1:T(8,128)S(1)}, u32[]{:S(2)}, u32[]{:S(2)}) collective-permute-start(f32[6,1,8,128]{3,2,0,1:T(8,128)S(1)} %slice.599), channel_id=1, source_target_pairs={{4,0},{8,4},{12,8},{0,12},{5,1},{9,5},{13,9},{1,13},{6,2},{10,6},{... | collective-permute-start | bytes 73736 | tf_op jit(solution)/shard_map/ppermute | solution.py:17
  9.8 2.2 %collective-permute-done.1 = f32[6,5,1,128]{3,2,0,1:T(1,128)S(1)} collective-permute-done((f32[6,5,1,128]{3,2,0,1:T(1,128)S(1)}, f32[6,5,1,128]{3,2,0,1:T(1,128)S(1)}, u32[]{:S(2)}, u32[]{:S(2)}) %collective-permute-start.1) | collective-permute-done | bytes 15392 | tf_op jit(solution)/shard_map/ppermute | solution.py:17
  13.8 131.3 %while.16 = (s32[]{:T(128)}, f32[6,5,9,129]{3,2,1,0:T(8,128)S(1)}, f32[2]{0:T(128)S(1)}, f32[6,5,9,129]{3,2,0,1:T(8,128)S(1)}, f32[3,3]{1,0:T(4,128)S(1)}, /*ind...) while((s32[]{:T(128)}, f32[6,5,9,129]{3,2,1,0:T(8,128)S(1)}, ...), condition=%wide.region_1.2_spmd.clone, body=%wide.region_0.1_spmd.sunk.clone.sunk | while | flops 26604940 | bytes 19892932 | solution.py:187
  14.7 1.7 slice.981
  16.4 1.7 slice.982
  26.6 7.0 %constant_dynamic-update-slice_fusion.35 = (f32[6,3,3,3,256]{4,1,3,2,0:T(4,128)S(1)}, f32[1,3,3,3,1,256]{5,1,3,2,4,0:T(4,128)S(1)}, f32[1,3,3,3,1,256]{5,1,3,2,4...) fusion(f32[]{:T(128)} %bitcast.376, f32[]{:T(128)} %bitcast.377, ...), kind=kLoop, calls=%fused_computation.67.clone.1 | loop fusion | flops 221183 | bytes 433196 | tf_op jit(solution)/shard_map/while
  33.6 4.4 %constant_dynamic-update-slice_fusion.36 = (f32[6,3,3,3,256]{4,1,3,2,0:T(4,128)S(1)}, f32[1,3,3,3,1,256]{5,1,3,2,4,0:T(4,128)S(1)}) fusion(f32[6,3,3,3,256]{4,1,3,2,0:T(4,128)S(1)} %get-tuple-element.384, f32[]{:T(128)} %bitcast.376, f32[]{:T(128)} %bitcast.388, f32[6,3,3,3,1,256]{5,1,3,2,4,0:T(4,128)S(1)} %convolution_bitcast_fusion.24, ...), kind=kLoop, calls=%fused_computation.66.clone.1 | loop fusion | flops 103680 | bytes 294940 | tf_op jit(solution)/shard_map/while
  38.0 4.6 %constant_dynamic-update-slice_fusion.37 = (f32[6,3,3,3,256]{4,1,3,2,0:T(4,128)S(1)}, f32[1,3,3,3,1,256]{5,1,3,2,4,0:T(4,128)S(1)}) fusion(f32[6,3,3,3,256]{4,1,3,2,0:T(4,128)S(1)} %get-tuple-element.386, f32[]{:T(128)} %bitcast.376, f32[]{:T(128)} %bitcast.385, f32[6,3,3,3,1,256]{5,1,3,2,4,0:T(4,128)S(1)} %convolution_bitcast_fusion.24, ...), kind=kLoop, calls=%fused_computation.65.clone.1 | loop fusion | flops 117504 | bytes 294940 | tf_op jit(solution)/shard_map/while
  42.6 7.1 %constant_dynamic-update-slice_fusion.38 = (f32[6,3,3,3,256]{4,1,3,2,0:T(4,128)S(1)}, f32[1,3,3,3,1,256]{5,1,3,2,4,0:T(4,128)S(1)}, f32[1,3,3,3,1,256]{5,1,3,2,4...) fusion(f32[6,3,3,3,256]{4,1,3,2,0:T(4,128)S(1)} %get-tuple-elem, ...), kind=kLoop, calls=%fused_computation.64.clone.1 | loop fusion | flops 483840 | bytes 1290284 | tf_op jit(solution)/shard_map/while
  52.5 2.0 %constant_dynamic-update-slice_fusion.39 = f32[6,3,3,3,256]{4,1,3,2,0:T(4,128)S(1)} fusion(f32[1,3,3,3,1,256]{5,1,3,2,4,0:T(4,128)S(1)} %get-tuple-element.393, f32[]{:T(128)} %bitcast.376, f32[]{:T(128)} %bitcast.382, f32[6,3,3,3,1,256]{5,1,3,2,4,0:T(4,128)S(1)} %convolution_bitcast_fusion.27, f32[1,3,3,3,1,256]{5,1,3,2,4,0:T(4,128)S(1)} %get-tuple-element.385, ...), kind=kLoop, calls=%fused_computation.61.clone.1 | loop fusion | flops 41471 | bytes 119820 | tf_op jit(solution)/shard_map/while
  54.5 2.0 %constant_dynamic-update-slice_fusion.40 = f32[6,3,3,3,256]{4,1,3,2,0:T(4,128)S(1)} fusion(f32[6,3,3,3,256]{4,1,3,2,0:T(4,128)S(1)} %constant_dynamic-update-slice_fusion.39, f32[1,3,3,3,1,256]{5,1,3,2,4,0:T(4,128)S(1)} %get-tuple-element.394, f32[]{:T(128)} %bitcast.376, f32[]{:T(128)} %bitcast.390, ...), kind=kLoop, calls=%fused_computation.60.clone.1 | loop fusion | flops 48384 | bytes 147468 | tf_op jit(solution)/shard_map/while
  56.5 2.0 %constant_dynamic-update-slice_fusion.41 = f32[6,3,3,3,256]{4,1,3,2,0:T(4,128)S(1)} fusion(f32[6,3,3,3,256]{4,1,3,2,0:T(4,128)S(1)} %constant_dynamic-update-slice_fusion.40, f32[1,3,3,3,1,256]{5,1,3,2,4,0:T(4,128)S(1)} %get-tuple-element.395, f32[]{:T(128)} %bitcast.376, f32[]{:T(128)} %bitcast.389, ...), kind=kLoop, calls=%fused_computation.59.clone.1 | loop fusion | flops 41472 | bytes 147468 | tf_op jit(solution)/shard_map/while
  58.5 1.9 %constant_dynamic-update-slice_fusion.42 = (f32[6,3,3,3,256]{4,1,3,2,0:T(4,128)S(1)}, f32[6,3,3,3,256]{4,1,3,2,0:T(4,128)S(1)}) fusion(f32[6,3,3,3,256]{4,1,3,2,0:T(4,128)S(1)} %constant_dynamic-update-slice_fusion.41, f32[1,3,3,3,1,256]{5,1,3,2,4,0:T(4,128)S(1)} %get-tuple-element.396, f32[1,3,3,3,1,256]{5,1,3,2,4,0:T(4,128)S(1)} %get-tuple-element.393, ...), kind=kLoop, calls=%fused_computation.58.clone.1 | loop fusion | flops 124415 | bytes 479244 | tf_op jit(solution)/shard_map/while
  60.4 2.1 %constant_dynamic-update-slice_fusion.44 = (f32[6,3,3,3,256]{4,1,3,2,0:T(4,128)S(1)}, f32[6,3,3,3,256]{4,1,3,2,0:T(4,128)S(1)}) fusion(f32[6,3,3,3,256]{4,1,3,2,0:T(4,128)S(1)} %get-tuple-element.401, f32[1,3,3,3,1,256]{5,1,3,2,4,0:T(4,128)S(1)} %get-tuple-element.396, f32[1,3,3,3,1,256]{5,1,3,2,4,0:T(4,128)S(1)} %get-tuple-element.394, ...), kind=kLoop, calls=%fused_computation.57.clone.1 | loop fusion | flops 152064 | bytes 552972 | tf_op jit(solution)/shard_map/while
  62.5 2.0 %constant_dynamic-update-slice_fusion.46 = (f32[6,3,3,3,256]{4,1,3,2,0:T(4,128)S(1)}, f32[6,3,3,3,256]{4,1,3,2,0:T(4,128)S(1)}) fusion(f32[6,3,3,3,256]{4,1,3,2,0:T(4,128)S(1)} %get-tuple-element.407, f32[1,3,3,3,1,256]{5,1,3,2,4,0:T(4,128)S(1)} %get-tuple-element.396, f32[1,3,3,3,1,256]{5,1,3,2,4,0:T(4,128)S(1)} %get-tuple-element.395, ...), kind=kLoop, calls=%fused_computation.56.clone.1 | loop fusion | flops 152064 | bytes 552972 | tf_op jit(solution)/shard_map/while/body/eval_jaxpr/stack | solution.py:151
  77.4 2.0 %copy.185 = f32[6,3,9,129]{3,2,1,0:T(8,128)S(1)} copy(f32[6,3,9,129]{2,3,1,0:T(8,128)} %slice_add_fusion.13) | data formatting | bytes 167184 | tf_op jit(solution)/shard_map/while/body/eval_jaxpr/dynamic_update_slice | solution.py:185
  80.3 1.7 slice.981
  82.0 1.7 slice.982
  92.3 7.0 %constant_dynamic-update-slice_fusion.35 = (f32[6,3,3,3,256]{4,1,3,2,0:T(4,128)S(1)}, f32[1,3,3,3,1,256]{5,1,3,2,4,0:T(4,128)S(1)}, f32[1,3,3,3,1,256]{5,1,3,2,4...) fusion(f32[]{:T(128)} %bitcast.376, f32[]{:T(128)} %bitcast.377, ...), kind=kLoop, calls=%fused_computation.67.clone.1 | loop fusion | flops 221183 | bytes 433196 | tf_op jit(solution)/shard_map/while
  99.3 4.4 %constant_dynamic-update-slice_fusion.36 = (f32[6,3,3,3,256]{4,1,3,2,0:T(4,128)S(1)}, f32[1,3,3,3,1,256]{5,1,3,2,4,0:T(4,128)S(1)}) fusion(f32[6,3,3,3,256]{4,1,3,2,0:T(4,128)S(1)} %get-tuple-element.384, f32[]{:T(128)} %bitcast.376, f32[]{:T(128)} %bitcast.388, f32[6,3,3,3,1,256]{5,1,3,2,4,0:T(4,128)S(1)} %convolution_bitcast_fusion.24, ...), kind=kLoop, calls=%fused_computation.66.clone.1 | loop fusion | flops 103680 | bytes 294940 | tf_op jit(solution)/shard_map/while
  103.7 4.6 %constant_dynamic-update-slice_fusion.37 = (f32[6,3,3,3,256]{4,1,3,2,0:T(4,128)S(1)}, f32[1,3,3,3,1,256]{5,1,3,2,4,0:T(4,128)S(1)}) fusion(f32[6,3,3,3,256]{4,1,3,2,0:T(4,128)S(1)} %get-tuple-element.386, f32[]{:T(128)} %bitcast.376, f32[]{:T(128)} %bitcast.385, f32[6,3,3,3,1,256]{5,1,3,2,4,0:T(4,128)S(1)} %convolution_bitcast_fusion.24, ...), kind=kLoop, calls=%fused_computation.65.clone.1 | loop fusion | flops 117504 | bytes 294940 | tf_op jit(solution)/shard_map/while
  108.2 7.1 %constant_dynamic-update-slice_fusion.38 = (f32[6,3,3,3,256]{4,1,3,2,0:T(4,128)S(1)}, f32[1,3,3,3,1,256]{5,1,3,2,4,0:T(4,128)S(1)}, f32[1,3,3,3,1,256]{5,1,3,2,4...) fusion(f32[6,3,3,3,256]{4,1,3,2,0:T(4,128)S(1)} %get-tuple-elem, ...), kind=kLoop, calls=%fused_computation.64.clone.1 | loop fusion | flops 483840 | bytes 1290284 | tf_op jit(solution)/shard_map/while
  118.2 2.0 %constant_dynamic-update-slice_fusion.39 = f32[6,3,3,3,256]{4,1,3,2,0:T(4,128)S(1)} fusion(f32[1,3,3,3,1,256]{5,1,3,2,4,0:T(4,128)S(1)} %get-tuple-element.393, f32[]{:T(128)} %bitcast.376, f32[]{:T(128)} %bitcast.382, f32[6,3,3,3,1,256]{5,1,3,2,4,0:T(4,128)S(1)} %convolution_bitcast_fusion.27, f32[1,3,3,3,1,256]{5,1,3,2,4,0:T(4,128)S(1)} %get-tuple-element.385, ...), kind=kLoop, calls=%fused_computation.61.clone.1 | loop fusion | flops 41471 | bytes 119820 | tf_op jit(solution)/shard_map/while
  120.2 2.0 %constant_dynamic-update-slice_fusion.40 = f32[6,3,3,3,256]{4,1,3,2,0:T(4,128)S(1)} fusion(f32[6,3,3,3,256]{4,1,3,2,0:T(4,128)S(1)} %constant_dynamic-update-slice_fusion.39, f32[1,3,3,3,1,256]{5,1,3,2,4,0:T(4,128)S(1)} %get-tuple-element.394, f32[]{:T(128)} %bitcast.376, f32[]{:T(128)} %bitcast.390, ...), kind=kLoop, calls=%fused_computation.60.clone.1 | loop fusion | flops 48384 | bytes 147468 | tf_op jit(solution)/shard_map/while
  122.2 2.0 %constant_dynamic-update-slice_fusion.41 = f32[6,3,3,3,256]{4,1,3,2,0:T(4,128)S(1)} fusion(f32[6,3,3,3,256]{4,1,3,2,0:T(4,128)S(1)} %constant_dynamic-update-slice_fusion.40, f32[1,3,3,3,1,256]{5,1,3,2,4,0:T(4,128)S(1)} %get-tuple-element.395, f32[]{:T(128)} %bitcast.376, f32[]{:T(128)} %bitcast.389, ...), kind=kLoop, calls=%fused_computation.59.clone.1 | loop fusion | flops 41472 | bytes 147468 | tf_op jit(solution)/shard_map/while
  124.2 1.9 %constant_dynamic-update-slice_fusion.42 = (f32[6,3,3,3,256]{4,1,3,2,0:T(4,128)S(1)}, f32[6,3,3,3,256]{4,1,3,2,0:T(4,128)S(1)}) fusion(f32[6,3,3,3,256]{4,1,3,2,0:T(4,128)S(1)} %constant_dynamic-update-slice_fusion.41, f32[1,3,3,3,1,256]{5,1,3,2,4,0:T(4,128)S(1)} %get-tuple-element.396, f32[1,3,3,3,1,256]{5,1,3,2,4,0:T(4,128)S(1)} %get-tuple-element.393, ...), kind=kLoop, calls=%fused_computation.58.clone.1 | loop fusion | flops 124415 | bytes 479244 | tf_op jit(solution)/shard_map/while
  126.1 2.1 %constant_dynamic-update-slice_fusion.44 = (f32[6,3,3,3,256]{4,1,3,2,0:T(4,128)S(1)}, f32[6,3,3,3,256]{4,1,3,2,0:T(4,128)S(1)}) fusion(f32[6,3,3,3,256]{4,1,3,2,0:T(4,128)S(1)} %get-tuple-element.401, f32[1,3,3,3,1,256]{5,1,3,2,4,0:T(4,128)S(1)} %get-tuple-element.396, f32[1,3,3,3,1,256]{5,1,3,2,4,0:T(4,128)S(1)} %get-tuple-element.394, ...), kind=kLoop, calls=%fused_computation.57.clone.1 | loop fusion | flops 152064 | bytes 552972 | tf_op jit(solution)/shard_map/while
  128.1 2.0 %constant_dynamic-update-slice_fusion.46 = (f32[6,3,3,3,256]{4,1,3,2,0:T(4,128)S(1)}, f32[6,3,3,3,256]{4,1,3,2,0:T(4,128)S(1)}) fusion(f32[6,3,3,3,256]{4,1,3,2,0:T(4,128)S(1)} %get-tuple-element.407, f32[1,3,3,3,1,256]{5,1,3,2,4,0:T(4,128)S(1)} %get-tuple-element.396, f32[1,3,3,3,1,256]{5,1,3,2,4,0:T(4,128)S(1)} %get-tuple-element.395, ...), kind=kLoop, calls=%fused_computation.56.clone.1 | loop fusion | flops 152064 | bytes 552972 | tf_op jit(solution)/shard_map/while/body/eval_jaxpr/stack | solution.py:151
  143.1 2.0 %copy.185 = f32[6,3,9,129]{3,2,1,0:T(8,128)S(1)} copy(f32[6,3,9,129]{2,3,1,0:T(8,128)} %slice_add_fusion.13) | data formatting | bytes 167184 | tf_op jit(solution)/shard_map/while/body/eval_jaxpr/dynamic_update_slice | solution.py:185
  148.5 2.2 %collective-permute-done.4 = f32[6,5,1,128]{3,2,1,0:T(1,128)S(1)} collective-permute-done((f32[6,5,1,128]{3,2,1,0:T(1,128)S(1)}, f32[6,5,1,128]{3,2,1,0:T(1,128)S(1)}, u32[]{:S(2)}, u32[]{:S(2)}) %collective-permute-start.4) | collective-permute-done | bytes 15392 | tf_op jit(solution)/shard_map/ppermute | solution.py:17
  151.3 5.6 %collective-permute-done.5 = f32[6,1,8,128]{3,2,1,0:T(8,128)S(1)} collective-permute-done((f32[6,1,8,128]{3,2,1,0:T(8,128)S(1)}, f32[6,1,8,128]{3,2,1,0:T(8,128)S(1)}, u32[]{:S(2)}, u32[]{:S(2)}) %collective-permute-start.5) | collective-permute-done | bytes 24608 | tf_op jit(solution)/shard_map/ppermute | solution.py:17
  158.2 30.6 %all-reduce.6 = (f32[]{:T(128)}, f32[]{:T(128)}) all-reduce(f32[]{:T(128)} %get-tuple-element.264, f32[]{:T(128)} %get-tuple-element.290), channel_id=1, replica_groups=mesh['body'=2,'gx'=4,'gy'=2,'gz'=2] {'gx','gy','gz'}, use_global_device_ids=true, to_apply=%region_5.6 | all-reduce | flops 2 | bytes 16 | tf_op jit(solution)/shard_map/psum | solution.py:216
  (151 shorter events, 61.0 us)
Async XLA Ops:
  0.6 13.2 %copy-start.2 = (f32[3,3,1,1,1]{1,0,4,3,2:T(4,128)S(1)}, f32[3,3,1,1,1]{1,0,4,3,2:T(4,128)}, u32[]{:S(2)}) copy-start(f32[3,3,1,1,1]{1,0,4,3,2:T(4,128)} %constant.292) | copy-start | bytes 112
  0.6 13.2 %copy-start.4 = (f32[3,3,1,1,1]{1,0,4,3,2:T(4,128)S(1)}, f32[3,3,1,1,1]{1,0,4,3,2:T(4,128)}, u32[]{:S(2)}) copy-start(f32[3,3,1,1,1]{1,0,4,3,2:T(4,128)} %constant.293) | copy-start | bytes 112
  0.7 13.1 %copy-start.3 = (f32[3,3,3]{0,2,1:T(4,128)S(1)}, f32[3,3,3]{0,2,1:T(4,128)}, u32[]{:S(2)}) copy-start(f32[3,3,3]{0,2,1:T(4,128)} %constant.74.clone..sunk.2) | copy-start | bytes 328
  0.7 13.1 %copy-start.7 = (f32[2]{0:T(128)S(1)}, f32[2]{0:T(128)}, u32[]{:S(2)}) copy-start(f32[2]{0:T(128)} %param.10) | copy-start | bytes 28
  0.7 13.1 %copy-start.5 = (f32[3,3]{1,0:T(4,128)S(1)}, f32[3,3]{1,0:T(4,128)}, u32[]{:S(2)}) copy-start(f32[3,3]{1,0:T(4,128)} %param.9) | copy-start | bytes 112
  1.6 6.7 %collective-permute-start = (f32[6,1,8,128]{3,2,0,1:T(8,128)S(1)}, f32[6,1,8,128]{3,2,0,1:T(8,128)S(1)}, u32[]{:S(2)}, u32[]{:S(2)}) collective-permute-start(f32[6,1,8,128]{3,2,0,1:T(8,128)S(1)} %slice.599), channel_id=1, source_target_pairs={{4,0},{8,4},{12,8},{0,12},{5,1},{9,5},{13,9},{1,13},{6,2},{10,6},{... | collective-permute-start | bytes 73736 | tf_op jit(solution)/shard_map/ppermute | solution.py:17
  8.3 3.8 %collective-permute-start.1 = (f32[6,5,1,128]{3,2,0,1:T(1,128)S(1)}, f32[6,5,1,128]{3,2,0,1:T(1,128)S(1)}, u32[]{:S(2)}, u32[]{:S(2)}) collective-permute-start(f32[6,5,1,128]{3,2,0,1:T(1,128)S(1)} %pad_maximum_fusion.8), channel_id=1, source_target_pairs={{2,0},{0,2},{3,1},{1,3},{6,4},{4,6},{7,5},{5,7},{10,8},{8,10},{11,... | collective-permute-start | bytes 46088 | tf_op jit(solution)/shard_map/ppermute | solution.py:17
  12.1 1.6 collective-permute-start.2
  13.8 0.8 copy-start
  77.4 2.1 %copy-start.1 = (f32[6,5,9,129]{3,2,0,1:T(8,128)S(1)}, f32[6,5,9,129]{3,2,0,1:T(8,128)}, u32[]{:S(2)}) copy-start(f32[6,5,9,129]{3,2,0,1:T(8,128)} %copy-done) | copy-start | bytes 417964 | tf_op jit(solution)/shard_map/while
  79.5 0.8 copy-start
  143.1 2.1 %copy-start.1 = (f32[6,5,9,129]{3,2,0,1:T(8,128)S(1)}, f32[6,5,9,129]{3,2,0,1:T(8,128)}, u32[]{:S(2)}) copy-start(f32[6,5,9,129]{3,2,0,1:T(8,128)} %copy-done) | copy-start | bytes 417964 | tf_op jit(solution)/shard_map/while
  145.2 1.6 collective-permute-start.3
  145.5 11.4 %copy-start.6 = (f32[2,3,4,8,128]{4,3,2,1,0:T(8,128)S(1)}, f32[2,3,4,8,128]{4,3,2,1,0:T(8,128)}, u32[]{:S(2)}) copy-start(f32[2,3,4,8,128]{4,3,2,1,0:T(8,128)} %param.8) | copy-start | bytes 294916
  146.9 3.8 %collective-permute-start.4 = (f32[6,5,1,128]{3,2,1,0:T(1,128)S(1)}, f32[6,5,1,128]{3,2,1,0:T(1,128)S(1)}, u32[]{:S(2)}, u32[]{:S(2)}) collective-permute-start(f32[6,5,1,128]{3,2,1,0:T(1,128)S(1)} %pad_maximum_fusion.7), channel_id=1, source_target_pairs={{2,0},{0,2},{3,1},{1,3},{6,4},{4,6},{7,5},{5,7},{10,8},{8,10},{11,... | collective-permute-start | bytes 46088 | tf_op jit(solution)/shard_map/ppermute | solution.py:17
  150.9 6.0 %collective-permute-start.5 = (f32[6,1,8,128]{3,2,1,0:T(8,128)S(1)}, f32[6,1,8,128]{3,2,1,0:T(8,128)S(1)}, u32[]{:S(2)}, u32[]{:S(2)}) collective-permute-start(f32[6,1,8,128]{3,2,1,0:T(8,128)S(1)} %slice.601), channel_id=1, source_target_pairs={{12,0},{0,4},{4,8},{8,12},{13,1},{1,5},{5,9},{9,13},{14,2},{2,6},{... | collective-permute-start | bytes 73736 | tf_op jit(solution)/shard_map/ppermute | solution.py:17
where the time goes:
time: 192 us; the launch traced here: 191 us
  other arithmetic  89.3 us (47%)
  blocking collectives  30.6 us (16%)
  local copies, waits for them, and re-layouts  27.5 us (14%)
  matrix products  17.3 us (9%)
  waiting for transfers between devices  14.4 us (8%)
  starting transfers between devices  8.83 us (5%)
  between operations  2.13 us (1%)
    while x24, other arithmetic  74.4 us
    psum x1, blocking collectives, local(): totals = lax.psum((squares, curvature), ('gx', 'gy', 'gz'))  30.6 us
    ppermute x6, waiting for transfers between devices, passed_along(): return lax.ppermute(block, axis, route)  14.4 us
    another operation x6, other arithmetic, layer_forces(): jnp.stack([stress[0][along], stress[1][along], stress[2][along], dstress[...  9.54 us
    ppermute x6, starting transfers between devices, passed_along(): return lax.ppermute(block, axis, route)  8.83 us
    dynamic_update_slice x4, local copies, waits for them, and re-layouts, one_layer(): lax.dynamic_update_slice_in_dim(accumulated, current + contribution, plan...  4.15 us
    slice x4, local copies, waits for them, and re-layouts, triplets(): odd_nodes = lax.slice_in_dim(array, 1, 2 * elements, 2, axis)  4.04 us
    slice x4, local copies, waits for them, and re-layouts, triplets(): next_nodes = lax.slice_in_dim(array, 2, 2 * elements + 1, 2, axis)  4.04 us
  transfers between devices with their start and end apart: 6, of which 6 were waited for; matrix products, arithmetic and copies ran while one was open for 0% of the time, Pallas kernels for 0%

commit v1 on v0

v1 whole, which is shorter than its diff:
```python
import functools
import math

import jax
import jax.numpy as jnp
import numpy as np
from jax import lax
from jax.experimental import pallas as pl
from jax.experimental.pallas import tpu as pltpu
from jax.sharding import PartitionSpec as P

MESH = pl.DeviceIdType.MESH
BF16 = jnp.bfloat16
F32 = jnp.float32
root_eps = 1e-06
XI = math.sqrt(0.6)
HALO = 2
POINTS = np.array([-XI, 0.0, XI])
VALUES = np.stack([POINTS * (POINTS - 1) / 2, 1 - POINTS**2, POINTS * (POINTS + 1) / 2], axis=1)
SLOPES = np.stack([POINTS - 0.5, -2 * POINTS, POINTS + 0.5], axis=1) * 0.5
WEIGHTS = np.array([5 / 9, 8 / 9, 5 / 9])


def split_const(matrix):
    hi = matrix.astype(jnp.bfloat16).astype(np.float64)
    return hi, (matrix - hi).astype(jnp.bfloat16).astype(np.float64)


def stacked(matrix, depth):
    hi, lo = split_const(matrix)
    pad = np.zeros((matrix.shape[0], depth - 3 * matrix.shape[1]))
    return np.concatenate([hi, hi, lo, pad], axis=1).astype(jnp.bfloat16)


def y_tables(ny):
    elements = ny // 2 + 1
    value = np.zeros((16, 16))
    slope = np.zeros((16, 16))
    for e in range(elements):
        for a in range(3):
            node = 2 * e - 2 + a
            slot = node if 0 <= node < ny else (ny + 2 + node if node < 0 else ny + 2)
            for q in range(3):
                value[3 * e + q, slot] += VALUES[q, a]
                slope[3 * e + q, slot] += SLOPES[q, a]
    return value, slope


def forward_matrix(ny):
    value, slope = y_tables(ny)
    out = np.zeros((3, 2, 3, 16, 5, 16))
    for e in range(2):
        for q in range(3):
            for a in range(3):
                out[0, e, q, :, 2 * e + a, :] += SLOPES[q, a] * value
                out[1, e, q, :, 2 * e + a, :] += VALUES[q, a] * slope
                out[2, e, q, :, 2 * e + a, :] += VALUES[q, a] * value
    return stacked(out.reshape(288, 80), 256)


def backward_matrix(ny):
    value, slope = y_tables(ny)
    weight = np.zeros((16, 1))
    for row in range(3 * (ny // 2 + 1)):
        weight[row] = 8 * WEIGHTS[row % 3]
    out = np.zeros((2, ny, 2, 2, 16))
    for plane in range(2):
        out[plane, :, plane, 0, :] = (value * weight)[:, :ny].T
        out[plane, :, plane, 1, :] = (slope * weight)[:, :ny].T
    return stacked(out.reshape(2 * ny, 64), 256)


def stress(f, df, lame_s):
    cof = [
        [
            f[(r + 1) % 3][(c + 1) % 3] * f[(r + 2) % 3][(c + 2) % 3]
            - f[(r + 1) % 3][(c + 2) % 3] * f[(r + 2) % 3][(c + 1) % 3]
            for c in range(3)
        ]
        for r in range(3)
    ]
    jac = f[0][0] * cof[0][0] + f[0][1] * cof[0][1] + f[0][2] * cof[0][2]
    inv = 1.0 / jac
    h = [[cof[r][c] * inv for c in range(3)] for r in range(3)]
    m = lame_s * jnp.log(jac) - 1.0
    p = [[f[r][c] + m * h[r][c] for c in range(3)] for r in range(3)]
    prod = [
        [h[r][0] * df[c][0] + h[r][1] * df[c][1] + h[r][2] * df[c][2] for c in range(3)]
        for r in range(3)
    ]
    trace = lame_s * (prod[0][0] + prod[1][1] + prod[2][2])
    mix = [
        [trace - m * prod[r][c] if r == c else -(m * prod[r][c]) for c in range(3)]
        for r in range(3)
    ]
    dp = [
        [
            df[r][c] + mix[r][0] * h[0][c] + mix[r][1] * h[1][c] + mix[r][2] * h[2][c]
            for c in range(3)
        ]
        for r in range(3)
    ]
    return p, dp


def z_value(a, b):
    c = pltpu.roll(a, 127, 1)
    base = 0.4 * b + 0.3 * (a + c)
    tilt = (XI / 2) * (c - a)
    return [base - tilt, b, base + tilt]


def z_slope(a, b):
    c = pltpu.roll(a, 127, 1)
    mid = 0.25 * (c - a)
    bend = (XI / 2) * (a + c - 2.0 * b)
    return [mid - bend, mid, mid + bend]


def z_value_back(f):
    w, w0 = WEIGHTS[0], WEIGHTS[1]
    plus, minus = f[2] + f[0], f[2] - f[0]
    side = (0.3 * w) * plus
    tilt = (XI / 2 * w) * minus
    return side - tilt, (0.4 * w) * plus + w0 * f[1], side + tilt


def z_slope_back(f):
    w, w0 = WEIGHTS[0], WEIGHTS[1]
    plus, minus = f[2] + f[0], f[2] - f[0]
    mid = (0.25 * w) * plus + (0.25 * w0) * f[1]
    bend = (XI / 2 * w) * minus
    return bend - mid, -2.0 * bend, bend + mid


def hi_lo(value):
    hi = value.astype(BF16)
    return hi, (value - hi.astype(F32)).astype(BF16)


def dot(a, b):
    return jnp.dot(a, b, preferred_element_type=F32)


def stat_stages(sizes):
    if sizes[0] * sizes[1] * sizes[2] <= 32:
        return [(True, True, True)]
    return [(False, True, True), (True, False, False)]


def stage_offsets(stage, sizes):
    ranges = [range(n) if used else range(1) for used, n in zip(stage, sizes)]
    return [(a, b, c) for a in ranges[0] for b in ranges[1] for c in ranges[2] if (a, b, c) != (0, 0, 0)]


def kernel(
    sizes, strain_ref, material_ref, fields_ref, fwd_hbm, bwd_hbm,
    res_ref, tan_ref, stats_ref,
    own, main, halo, fwd, bwd, perm, perm_t, ybuf, acc, back, result, sums, partial,
    local_sem, send_sem, recv_sem, out_sem, stat_send, stat_recv,
):
    nx, ny, nz = sizes
    gx, gy, gz = lax.axis_index("gx"), lax.axis_index("gy"), lax.axis_index("gz")

    def device(ox, oy, oz):
        return {
            "gx": lax.rem(gx + ox % nx, nx),
            "gy": lax.rem(gy + oy % ny, ny),
            "gz": lax.rem(gz + oz % nz, nz),
        }

    stages = stat_stages(sizes)
    greet = {
        (ox % nx, oy % ny, oz) for ox in (-1, 0, 1) for oy in (-1, 0, 1) for oz in (0, 1)
    }
    for stage in stages:
        greet |= set(stage_offsets(stage, sizes))
    greet -= {(0, 0, 0)}
    barrier = pltpu.get_barrier_semaphore()
    for offset in sorted(greet):
        pl.semaphore_signal(barrier, inc=1, device_id=device(*offset), device_id_type=MESH)

    lanes = pl.ds(pl.multiple_of(gz * 128, 128), 128)
    get_own = pltpu.make_async_copy(fields_ref, own, local_sem.at[0])
    get_own.start()
    def keep(core):
        first, count = (2, 3) if core == 0 else (0, 4)
        return pltpu.make_async_copy(
            fields_ref.at[:, pl.ds(0, count)], main.at[:, pl.ds(first, count), :, lanes], local_sem.at[1]
        )

    for core in range(2):
        @pl.when(gz == core)
        def _():
            keep(core).start()
    get_fwd = pltpu.make_async_copy(fwd_hbm, fwd, local_sem.at[2])
    get_fwd.start()
    get_bwd = pltpu.make_async_copy(bwd_hbm, bwd, local_sem.at[3])
    get_bwd.start()

    rows = lax.broadcasted_iota(jnp.int32, (256, 256), 0)
    cols = lax.broadcasted_iota(jnp.int32, (256, 256), 1)
    perm[...] = (rows == jnp.where(cols < 128, 2 * cols, 2 * cols - 255)).astype(F32).astype(BF16)
    perm_t[...] = (cols == jnp.where(rows < 128, 2 * rows, 2 * rows - 255)).astype(F32).astype(BF16)

    get_own.wait()
    pl.semaphore_wait(barrier, len(greet))

    kinds = [(1, 0, 2, 2, 0), (-1, 1, 0, 1, 4), (0, 0, 0, 3, 2), (0, 1, 0, 4, 0)]

    def message(kind, dy, sender, target):
        _, _, plane, count, slot = kinds[kind]
        at = pl.ds(pl.multiple_of(sender * 128, 128), 128)
        side = 0 if kind < 2 else 1
        index = side * 6 + (dy + 1) * 2 + sender
        src_rows, dst = {
            0: (pl.ds(0, 8), main.at[:, pl.ds(slot, count), :, at]),
            1: (pl.ds(6, 2), halo.at[:, pl.ds(slot, count), pl.ds(0, 2), at]),
            -1: (pl.ds(0, 1), halo.at[:, pl.ds(slot, count), pl.ds(2, 1), at]),
        }[dy]
        return pltpu.make_async_remote_copy(
            src_ref=own.at[:, pl.ds(plane, count), src_rows],
            dst_ref=dst,
            send_sem=send_sem.at[kind * 3 + dy + 1],
            recv_sem=recv_sem.at[index],
            device_id=target,
            device_id_type=MESH,
        )

    def outgoing(kind, dy):
        dx, core = kinds[kind][:2]
        target = {
            "gx": lax.rem(gx + dx % nx, nx), "gy": lax.rem(gy + dy % ny, ny),
            "gz": jnp.int32(core) if core else gz * 0,
        }
        return message(kind, dy, gz, target)

    plan = [(k, dy) for k in (0, 1) for dy in (1, -1, 0)] + [(k, dy) for k in (2, 3) for dy in (1, -1)]
    for kind, dy in plan:
        outgoing(kind, dy).start()
    for core in range(2):
        @pl.when(gz == core)
        def _():
            outgoing(3 - core, 0).start()

    for core in range(2):
        @pl.when(gz == core)
        def _():
            keep(core).wait()
            me = {"gx": gx, "gy": gy, "gz": gz}
            for sender in range(2):
                for dy in (0, 1, -1):
                    if dy != 0 or sender != core:
                        message(2 + core, dy, sender, me).wait_recv()
            for sender in range(2):
                for dy in (0, 1, -1):
                    message(core, dy, sender, me).wait_recv()
    get_fwd.wait()
    get_bwd.wait()

    used = lax.broadcasted_iota(jnp.int32, (8, 256), 0) < 3
    for c in range(6):
        tiles = []
        for p in range(5):
            tiles += [main[c, p], jnp.where(used, halo[c, p], 0.0)]
        hi, lo = hi_lo(jnp.concatenate(tiles, axis=0))
        hi, lo = (dot(part, perm[...]).astype(BF16) for part in (hi, lo))
        data = jnp.concatenate([hi, lo, hi, jnp.zeros((16, 256), BF16)], axis=0)
        ybuf[c] = dot(fwd[...], data)

    shear, lame = material_ref[0], material_ref[1]
    lame_s = lame / shear
    offset = [
        [strain_ref[r, c] + (1.0 if r == c else 0.0) for c in range(3)] for r in range(3)
    ]
    for half in range(2):
        for e in range(2):
            for q in range(3):
                base = (e * 3 + q) * 16 + half * 8
                grads = []
                for c in range(6):
                    def ab(kind):
                        row = pl.ds(kind * 96 + base, 8)
                        return ybuf[c, row, 0:128], ybuf[c, row, 128:256]
                    grads.append([z_value(*ab(0)), z_value(*ab(1)), z_slope(*ab(2))])
                for qz in range(3):
                    f = [[grads[r][d][qz] + offset[r][d] for d in range(3)] for r in range(3)]
                    df = [[grads[3 + r][d][qz] for d in range(3)] for r in range(3)]
                    p, dp = stress(f, df, lame_s)
                    flux = p + dp
                    for c in range(6):
                        for plane in range(2):
                            if e == 0 and plane == 1:
                                continue
                            a = 2 if e == 0 else plane
                            for d in range(3):
                                k = float((SLOPES if d == 0 else VALUES)[q, a] * WEIGHTS[q])
                                where = (half, c, plane, d, qz)
                                first = (e == 0 and q == 0) if plane == 0 else (e == 1 and q == 0)
                                if first:
                                    acc[where] = k * flux[c][d]
                                elif k != 0.0:
                                    acc[where] += k * flux[c][d]
        for c in range(6):
            for plane in range(2):
                def at(d):
                    return [acc[half, c, plane, d, qz] for qz in range(3)]
                xa, xb, xc = z_value_back(at(0))
                ya, yb, yc = z_value_back(at(1))
                za, zb, zc = z_slope_back(at(2))
                row = pl.ds(plane * 32 + half * 8, 8)
                back[c, row, 0:128] = xa + za + pltpu.roll(xc + zc, 1, 1)
                back[c, row, 128:256] = xb + zb
                row = pl.ds(plane * 32 + 16 + half * 8, 8)
                back[c, row, 0:128] = ya + pltpu.roll(yc, 1, 1)
                back[c, row, 128:256] = yb

    nodal = []
    for c in range(6):
        hi, lo = hi_lo(back[c])
        data = jnp.concatenate([hi, lo, hi, jnp.zeros((64, 256), BF16)], axis=0)
        nodal.append(dot(bwd[...], data))
    hi, lo = hi_lo(jnp.concatenate(nodal, axis=0) * shear)
    both = dot(hi, perm_t[...]) + dot(lo, perm_t[...])
    squares = jnp.zeros((8, 256), F32)
    curvature = jnp.zeros((8, 256), F32)
    for c in range(6):
        for plane in range(2):
            value = both[c * 16 + plane * 8:c * 16 + plane * 8 + 8]
            result[c, plane] = value
            if c < 3:
                squares += value * value
            else:
                curvature += main[c, 2 + plane] * value
    partial[0:1] = jnp.sum(squares[:, :128] + squares[:, 128:], axis=0, keepdims=True)
    partial[1:2] = jnp.sum(curvature[:, :128] + curvature[:, 128:], axis=0, keepdims=True)

    pending = []
    base = 0
    for number, stage in enumerate(stages):
        offsets = stage_offsets(stage, sizes)
        sends = []
        for index, off in enumerate(offsets):
            copy = pltpu.make_async_remote_copy(
                src_ref=partial, dst_ref=sums.at[base + index],
                send_sem=stat_send.at[base + index], recv_sem=stat_recv.at[base + index],
                device_id=device(*off), device_id_type=MESH,
            )
            copy.start()
            sends.append(copy)
        if number == 0:
            planes = pl.ds(gz * 2, 2)
            other = pl.ds(pl.multiple_of((1 - gz) * 128, 128), 128)
            for n, out in enumerate((res_ref, tan_ref)):
                part = result.at[pl.ds(3 * n, 3)]
                near = pltpu.make_async_copy(part.at[:, :, :, lanes], out.at[:, planes], out_sem.at[n])
                near.start()
                far = pltpu.make_async_remote_copy(
                    src_ref=part.at[:, :, :, other], dst_ref=out.at[:, planes],
                    send_sem=out_sem.at[2 + n], recv_sem=out_sem.at[4 + n],
                    device_id=device(0, 0, 1), device_id_type=MESH,
                )
                far.start()
                pending += [near, far]
        total = partial[...]
        for copy in sends:
            copy.wait()
        for index in range(len(offsets)):
            total += sums[base + index]
        if number + 1 < len(stages):
            partial[...] = total
        base += len(offsets)

    entries = 3.0 * (4 * nx) * (8 * ny) * (128 * nz)
    whole = jnp.sum(total, axis=1, keepdims=True) * (1.0 / entries)
    whole = jnp.broadcast_to(whole, (2, 128))
    rms = jnp.sqrt(whole + root_eps)
    stats_ref[0] = rms[0, 0]
    stats_ref[1] = whole[1, 0]

    for copy in pending:
        copy.wait()
    for kind, dy in plan:
        outgoing(kind, dy).wait_send()
    for core in range(2):
        @pl.when(gz == core)
        def _():
            outgoing(3 - core, 0).wait_send()


def local(sizes, fields, macro_strain, material):
    block = fields.shape[2:]
    flat = fields.reshape((6,) + block)
    shape = jax.ShapeDtypeStruct((3,) + block, F32)
    fwd = jnp.asarray(forward_matrix(block[1]))
    bwd = jnp.asarray(backward_matrix(block[1]))
    count = sum(len(stage_offsets(stage, sizes)) for stage in stat_stages(sizes))
    vmem, dma = pltpu.VMEM, pltpu.SemaphoreType.DMA
    anywhere = pl.BlockSpec(memory_space=pl.ANY)
    smem = pl.BlockSpec(memory_space=pltpu.SMEM)
    return pl.pallas_call(
        functools.partial(kernel, sizes),
        out_shape=(shape, shape, jax.ShapeDtypeStruct((2,), F32)),
        in_specs=[smem, smem, anywhere, anywhere, anywhere],
        out_specs=(anywhere, anywhere, smem),
        scratch_shapes=[
            vmem((6,) + block, F32),
            vmem((6, 5, 8, 256), F32),
            vmem((6, 5, 8, 256), F32),
            vmem((288, 256), BF16),
            vmem((16, 256), BF16),
            vmem((256, 256), BF16),
            vmem((256, 256), BF16),
            vmem((6, 288, 256), F32),
            vmem((2, 6, 2, 3, 3, 8, 128), F32),
            vmem((6, 64, 256), F32),
            vmem((6, 2, 8, 256), F32),
            vmem((count, 2, 128), F32),
            vmem((2, 128), F32),
            dma((4,)),
            dma((12,)),
            dma((12,)),
            dma((6,)),
            dma((count,)),
            dma((count,)),
        ],
        compiler_params=pltpu.CompilerParams(collective_id=0, has_side_effects=True),
    )(macro_strain, material, flat, fwd, bwd)


def solution(mesh):
    sizes = tuple(mesh.shape[name] for name in ("gx", "gy", "gz"))
    in_specs = (P("body", None, "gx", "gy", "gz"), P("body", None), P("body"))
    out_specs = (P("body", "gx", "gy", "gz"), P("body", "gx", "gy", "gz"), P("body"))
    return jax.shard_map(
        functools.partial(local, sizes),
        mesh=mesh, in_specs=in_specs, out_specs=out_specs, check_vma=False,
    )
```

time: 192 us -> 22.4 us (0.12)
  other arithmetic: 89.3 us -> 0 us
  blocking collectives: 30.6 us -> 0 us
  local copies, waits for them, and re-layouts: 27.5 us -> 2.61 us
  Pallas kernels: 0 us -> 18.9 us
  matrix products: 17.3 us -> 0 us
  waiting for transfers between devices: 14.4 us -> 0 us
  starting transfers between devices: 8.83 us -> 0 us
    while x24 -> x0, other arithmetic: 74.4 us -> none
    psum x1 -> x0, blocking collectives: 30.6 us -> none  [local(): totals = lax.psum((squares, curvature), ('gx', 'gy', 'gz'))]
    pallas_call x0 -> x1, Pallas kernels: none -> 18.9 us  [local(): pl.pallas_call(functools.partial(kernel, sizes), out_shape=(shape, shape,...]
    dot_general x32 -> x0, matrix products: 17.3 us -> none  [the longest x2 1.19 us: layer_forces(): jnp.einsum('qa,cqyzij->cayzij', values, fluxes[2], precision=highest)]
    slice x21 -> x0, local copies, waits for them, and re-layouts: 14.7 us -> none  [the longest x4 4.04 us: triplets(): odd_nodes = lax.slice_in_dim(array, 1, 2 * elements, 2, axis)]
    ppermute x6 -> x0, waiting for transfers between devices: 14.4 us -> none  [passed_along(): return lax.ppermute(block, axis, route)]
    another operation x17 -> x0, other arithmetic: 10.7 us -> none  [the longest x6 9.54 us: layer_forces(): jnp.stack([stress[0][along], stress[1][along], stress[2][along], dstress[...]
    ppermute x6 -> x0, starting transfers between devices: 8.83 us -> none  [passed_along(): return lax.ppermute(block, axis, route)]
  transfers between devices with their start and end apart: 6 -> 0, of which waited for: 6 -> 0; matrix products, arithmetic and copies ran while one was open for 0% -> 0% of each run, Pallas kernels for 0% -> 0%
where the time goes in v1:
time: 22.4 us; the launch traced here: 22.2 us
  Pallas kernels  18.9 us (84%)
  local copies, waits for them, and re-layouts  2.61 us (12%)
  between operations  0.65 us (3%)
    pallas_call x1, Pallas kernels, local(): pl.pallas_call(functools.partial(kernel, sizes), out_shape=(shape, shape,...  18.9 us
    unnamed x7, local copies, waits for them, and re-layouts  2.61 us

profile of v1, /device:TPU:0, one launch (start us, length us, event | category | flops | bytes accessed | tf_op | source)
XLA Modules:
  0.0 22.2 jit_solution(8372638834486162853)
XLA Ops:
  0.6 18.9 %shard_map.76 = (f32[3,4,8,128]{3,2,1,0:T(8,128)}, f32[3,4,8,128]{3,2,1,0:T(8,128)}, f32[2]{0:T(128)}) custom-call(f32[3,3]{1,0:T(4,128)} %strain_ref.1, f32[2]{0:T(128)} %material_ref.1, f32[6,4,8,128]{3,2,1,0:T(8,128)} %bitcast.1, bf16[288,256]{1,0:T(8,128)(2,1)} %constant.4.clone.fwd_hbm, bf16[16,256]{1,0:T(8,128)(2,1)} %constant.5.clone.bwd_hbm), custom_call_target="tpu_custom_call" | custom-call | tf_op jit(solution)/shard_map/pallas_call | solution.py:401
  19.6 0.0 copy-start
  19.6 1.4 %copy.11 = f32[3,4,8,128]{3,2,1,0:T(8,128)} copy(f32[3,4,8,128]{3,2,1,0:T(8,128)} %get-tuple-element.6) | data formatting | bytes 98304
  21.0 0.0 copy-done
  21.0 0.0 copy-start.1
  21.0 0.6 %copy.12 = f32[3,4,8,128]{3,2,1,0:T(8,128)} copy(f32[3,4,8,128]{3,2,1,0:T(8,128)S(1)} %copy-done) | data formatting | bytes 98304
  21.7 0.0 copy-done.1
  21.7 0.5 %copy.13 = f32[2]{0:T(128)} copy(f32[2]{0:T(128)S(1)} %copy-done.1) | data formatting | bytes 16
Async XLA Ops:
  19.6 1.4 %copy-start = (f32[3,4,8,128]{3,2,1,0:T(8,128)S(1)}, f32[3,4,8,128]{3,2,1,0:T(8,128)}, u32[]{:S(2)}) copy-start(f32[3,4,8,128]{3,2,1,0:T(8,128)} %get-tuple-element.7) | copy-start | bytes 147460
  21.0 0.7 %copy-start.1 = (f32[2]{0:T(128)S(1)}, f32[2]{0:T(128)}, u32[]{:S(2)}) copy-start(f32[2]{0:T(128)} %get-tuple-element.8) | copy-start | bytes 28

commit v2 on v1

--- a/solution.py
+++ b/solution.py
@@ -48,14 +48,13 @@
 
 def forward_matrix(ny):
     value, slope = y_tables(ny)
-    out = np.zeros((3, 2, 3, 16, 5, 16))
-    for e in range(2):
-        for q in range(3):
-            for a in range(3):
-                out[0, e, q, :, 2 * e + a, :] += SLOPES[q, a] * value
-                out[1, e, q, :, 2 * e + a, :] += VALUES[q, a] * slope
-                out[2, e, q, :, 2 * e + a, :] += VALUES[q, a] * value
-    return stacked(out.reshape(288, 80), 256)
+    out = np.zeros((3, 3, 16, 3, 16))
+    for q in range(3):
+        for a in range(3):
+            out[0, q, :, a, :] += SLOPES[q, a] * value
+            out[1, q, :, a, :] += VALUES[q, a] * slope
+            out[2, q, :, a, :] += VALUES[q, a] * value
+    return stacked(out.reshape(144, 48), 256)
 
 
 def backward_matrix(ny):
@@ -156,7 +155,7 @@
 def kernel(
     sizes, strain_ref, material_ref, fields_ref, fwd_hbm, bwd_hbm,
     res_ref, tan_ref, stats_ref,
-    own, main, halo, fwd, bwd, perm, perm_t, ybuf, acc, back, result, sums, partial,
+    own, main, halo, fwd, bwd, perm, perm_t, ybuf, acc, back, curve, result, sums, partial,
     local_sem, send_sem, recv_sem, out_sem, stat_send, stat_recv,
 ):
     nx, ny, nz = sizes
@@ -243,44 +242,32 @@
         def _():
             outgoing(3 - core, 0).start()
 
-    for core in range(2):
-        @pl.when(gz == core)
-        def _():
-            keep(core).wait()
-            me = {"gx": gx, "gy": gy, "gz": gz}
-            for sender in range(2):
-                for dy in (0, 1, -1):
-                    if dy != 0 or sender != core:
-                        message(2 + core, dy, sender, me).wait_recv()
-            for sender in range(2):
-                for dy in (0, 1, -1):
-                    message(core, dy, sender, me).wait_recv()
     get_fwd.wait()
     get_bwd.wait()
-
-    used = lax.broadcasted_iota(jnp.int32, (8, 256), 0) < 3
-    for c in range(6):
-        tiles = []
-        for p in range(5):
-            tiles += [main[c, p], jnp.where(used, halo[c, p], 0.0)]
-        hi, lo = hi_lo(jnp.concatenate(tiles, axis=0))
-        hi, lo = (dot(part, perm[...]).astype(BF16) for part in (hi, lo))
-        data = jnp.concatenate([hi, lo, hi, jnp.zeros((16, 256), BF16)], axis=0)
-        ybuf[c] = dot(fwd[...], data)
-
     shear, lame = material_ref[0], material_ref[1]
     lame_s = lame / shear
     offset = [
         [strain_ref[r, c] + (1.0 if r == c else 0.0) for c in range(3)] for r in range(3)
     ]
-    for half in range(2):
-        for e in range(2):
+    used = lax.broadcasted_iota(jnp.int32, (8, 256), 0) < 3
+
+    def element(e, opening):
+        for c in range(6):
+            tiles = []
+            for p in range(2 * e, 2 * e + 3):
+                tiles += [main[c, p], jnp.where(used, halo[c, p], 0.0)]
+            hi, lo = hi_lo(jnp.concatenate(tiles, axis=0))
+            hi, lo = (dot(part, perm[...]).astype(BF16) for part in (hi, lo))
+            data = jnp.concatenate([hi, lo, hi, jnp.zeros((112, 256), BF16)], axis=0)
+            ybuf[c] = dot(fwd[...], data)
+        for half in range(2):
+            energy = 0.0
             for q in range(3):
-                base = (e * 3 + q) * 16 + half * 8
+                base = q * 16 + half * 8
                 grads = []
                 for c in range(6):
                     def ab(kind):
-                        row = pl.ds(kind * 96 + base, 8)
+                        row = pl.ds(kind * 48 + base, 8)
                         return ybuf[c, row, 0:128], ybuf[c, row, 128:256]
                     grads.append([z_value(*ab(0)), z_value(*ab(1)), z_slope(*ab(2))])
                 for qz in range(3):
@@ -288,52 +275,73 @@
                     df = [[grads[3 + r][d][qz] for d in range(3)] for r in range(3)]
                     p, dp = stress(f, df, lame_s)
                     flux = p + dp
+                    if e == 1:
+                        work = sum(dp[r][d] * df[r][d] for r in range(3) for d in range(3))
+                        energy += float(8 * WEIGHTS[q] * WEIGHTS[qz]) * work
                     for c in range(6):
-                        for plane in range(2):
-                            if e == 0 and plane == 1:
-                                continue
+                        for plane in range(e + 1):
                             a = 2 if e == 0 else plane
                             for d in range(3):
                                 k = float((SLOPES if d == 0 else VALUES)[q, a] * WEIGHTS[q])
                                 where = (half, c, plane, d, qz)
-                                first = (e == 0 and q == 0) if plane == 0 else (e == 1 and q == 0)
-                                if first:
+                                if q == 0 and (opening or plane == 1):
                                     acc[where] = k * flux[c][d]
-                                elif k != 0.0:
+                                elif abs(k) > 1e-12:
                                     acc[where] += k * flux[c][d]
-        for c in range(6):
+            if e == 1:
+                curve[half] = energy
+
+    for core in range(2):
+        @pl.when(gz == core)
+        def _():
+            me = {"gx": gx, "gy": gy, "gz": gz}
+            keep(core).wait()
+            for sender in range(2):
+                for dy in (0, 1, -1):
+                    if dy != 0 or sender != core:
+                        message(2 + core, dy, sender, me).wait_recv()
+            element(1 - core, True)
+            for sender in range(2):
+                for dy in (0, 1, -1):
+                    message(core, dy, sender, me).wait_recv()
+            element(core, False)
+
+    def gather(field):
+        nodal = []
+        for c in range(3 * field, 3 * field + 3):
             for plane in range(2):
-                def at(d):
-                    return [acc[half, c, plane, d, qz] for qz in range(3)]
-                xa, xb, xc = z_value_back(at(0))
-                ya, yb, yc = z_value_back(at(1))
-                za, zb, zc = z_slope_back(at(2))
-                row = pl.ds(plane * 32 + half * 8, 8)
-                back[c, row, 0:128] = xa + za + pltpu.roll(xc + zc, 1, 1)
-                back[c, row, 128:256] = xb + zb
-                row = pl.ds(plane * 32 + 16 + half * 8, 8)
-                back[c, row, 0:128] = ya + pltpu.roll(yc, 1, 1)
-                back[c, row, 128:256] = yb
-
-    nodal = []
-    for c in range(6):
-        hi, lo = hi_lo(back[c])
-        data = jnp.concatenate([hi, lo, hi, jnp.zeros((64, 256), BF16)], axis=0)
-        nodal.append(dot(bwd[...], data))
-    hi, lo = hi_lo(jnp.concatenate(nodal, axis=0) * shear)
-    both = dot(hi, perm_t[...]) + dot(lo, perm_t[...])
-    squares = jnp.zeros((8, 256), F32)
-    curvature = jnp.zeros((8, 256), F32)
-    for c in range(6):
-        for plane in range(2):
-            value = both[c * 16 + plane * 8:c * 16 + plane * 8 + 8]
-            result[c, plane] = value
-            if c < 3:
-                squares += value * value
-            else:
-                curvature += main[c, 2 + plane] * value
-    partial[0:1] = jnp.sum(squares[:, :128] + squares[:, 128:], axis=0, keepdims=True)
-    partial[1:2] = jnp.sum(curvature[:, :128] + curvature[:, 128:], axis=0, keepdims=True)
+                for half in range(2):
+                    def at(d):
+                        return [acc[half, c, plane, d, qz] for qz in range(3)]
+                    xa, xb, xc = z_value_back(at(0))
+                    ya, yb, yc = z_value_back(at(1))
+                    za, zb, zc = z_slope_back(at(2))
+                    row = pl.ds(plane * 32 + half * 8, 8)
+                    back[c, row, 0:128] = xa + za + pltpu.roll(xc + zc, 1, 1)
+                    back[c, row, 128:256] = xb + zb
+                    row = pl.ds(plane * 32 + 16 + half * 8, 8)
+                    back[c, row, 0:128] = ya + pltpu.roll(yc, 1, 1)
+                    back[c, row, 128:256] = yb
+            hi, lo = hi_lo(back[c])
+            data = jnp.concatenate([hi, lo, hi, jnp.zeros((64, 256), BF16)], axis=0)
+            nodal.append(dot(bwd[...], data))
+        hi, lo = hi_lo(jnp.concatenate(nodal, axis=0) * shear)
+        both = dot(hi, perm_t[...]) + dot(lo, perm_t[...])
+        for c in range(3):
+            for plane in range(2):
+                result[3 * field + c, plane] = both[c * 16 + plane * 8:c * 16 + plane * 8 + 8]
+        return nodal
+
+    squares = sum(part[8 * n:8 * n + 8] * part[8 * n:8 * n + 8] for part in gather(0) for n in range(2))
+    squares = (shear * shear) * (squares[:, :128] + squares[:, 128:])
+    curvature = jnp.zeros((8, 128), F32)
+    for half in range(2):
+        point = lax.broadcasted_iota(jnp.int32, (8, 128), 0) + 8 * half
+        weight = jnp.where(lax.rem(point, 3) == 1, float(WEIGHTS[1]), float(WEIGHTS[0]))
+        weight = jnp.where((point >= 3) & (point < 3 * (own.shape[2] // 2 + 1)), weight, 0.0)
+        curvature += weight * curve[half]
+    partial[0:1] = jnp.sum(squares, axis=0, keepdims=True)
+    partial[1:2] = shear * jnp.sum(curvature, axis=0, keepdims=True)
 
     pending = []
     base = 0
@@ -349,19 +357,19 @@
             copy.start()
             sends.append(copy)
         if number == 0:
+            gather(1)
             planes = pl.ds(gz * 2, 2)
             other = pl.ds(pl.multiple_of((1 - gz) * 128, 128), 128)
             for n, out in enumerate((res_ref, tan_ref)):
                 part = result.at[pl.ds(3 * n, 3)]
-                near = pltpu.make_async_copy(part.at[:, :, :, lanes], out.at[:, planes], out_sem.at[n])
-                near.start()
                 far = pltpu.make_async_remote_copy(
                     src_ref=part.at[:, :, :, other], dst_ref=out.at[:, planes],
-                    send_sem=out_sem.at[2 + n], recv_sem=out_sem.at[4 + n],
+                    send_sem=out_sem.at[n], recv_sem=out_sem.at[2 + n],
                     device_id=device(0, 0, 1), device_id_type=MESH,
                 )
                 far.start()
-                pending += [near, far]
+                pending.append(far)
+                out[:, planes] = part[:, :, :, lanes]
         total = partial[...]
         for copy in sends:
             copy.wait()
@@ -371,13 +379,7 @@
             partial[...] = total
         base += len(offsets)
 
-    entries = 3.0 * (4 * nx) * (8 * ny) * (128 * nz)
-    whole = jnp.sum(total, axis=1, keepdims=True) * (1.0 / entries)
-    whole = jnp.broadcast_to(whole, (2, 128))
-    rms = jnp.sqrt(whole + root_eps)
-    stats_ref[0] = rms[0, 0]
-    stats_ref[1] = whole[1, 0]
-
+    stats_ref[...] = total
     for copy in pending:
         copy.wait()
     for kind, dy in plan:
@@ -386,6 +388,19 @@
         @pl.when(gz == core)
         def _():
             outgoing(3 - core, 0).wait_send()
+
+
+def finish(entries, res, tan, total, res_ref, tan_ref, stats_ref, sem):
+    copies = [pltpu.make_async_copy(res, res_ref, sem.at[0]), pltpu.make_async_copy(tan, tan_ref, sem.at[1])]
+    for copy in copies:
+        copy.start()
+    whole = jnp.sum(total[...], axis=1, keepdims=True) * (1.0 / entries)
+    whole = jnp.broadcast_to(whole, (2, 128))
+    rms = jnp.sqrt(whole + root_eps)
+    stats_ref[0] = rms[0, 0]
+    stats_ref[1] = whole[1, 0]
+    for copy in copies:
+        copy.wait()
 
 
 def local(sizes, fields, macro_strain, material):
@@ -398,34 +413,44 @@
     vmem, dma = pltpu.VMEM, pltpu.SemaphoreType.DMA
     anywhere = pl.BlockSpec(memory_space=pl.ANY)
     smem = pl.BlockSpec(memory_space=pltpu.SMEM)
-    return pl.pallas_call(
+    near = pl.BlockSpec(memory_space=vmem)
+    res, tan, total = pl.pallas_call(
         functools.partial(kernel, sizes),
-        out_shape=(shape, shape, jax.ShapeDtypeStruct((2,), F32)),
+        out_shape=(vmem(shape.shape, F32), vmem(shape.shape, F32), vmem((2, 128), F32)),
         in_specs=[smem, smem, anywhere, anywhere, anywhere],
-        out_specs=(anywhere, anywhere, smem),
+        out_specs=(near, near, near),
         scratch_shapes=[
             vmem((6,) + block, F32),
             vmem((6, 5, 8, 256), F32),
             vmem((6, 5, 8, 256), F32),
-            vmem((288, 256), BF16),
+            vmem((144, 256), BF16),
             vmem((16, 256), BF16),
             vmem((256, 256), BF16),
             vmem((256, 256), BF16),
-            vmem((6, 288, 256), F32),
+            vmem((6, 144, 256), F32),
             vmem((2, 6, 2, 3, 3, 8, 128), F32),
             vmem((6, 64, 256), F32),
+            vmem((2, 8, 128), F32),
             vmem((6, 2, 8, 256), F32),
             vmem((count, 2, 128), F32),
             vmem((2, 128), F32),
             dma((4,)),
             dma((12,)),
             dma((12,)),
-            dma((6,)),
+            dma((4,)),
             dma((count,)),
             dma((count,)),
         ],
         compiler_params=pltpu.CompilerParams(collective_id=0, has_side_effects=True),
     )(macro_strain, material, flat, fwd, bwd)
+    entries = 3.0 * math.prod(n * m for n, m in zip(block, sizes))
+    return pl.pallas_call(
+        functools.partial(finish, entries),
+        out_shape=(shape, shape, jax.ShapeDtypeStruct((2,), F32)),
+        in_specs=[near, near, near],
+        out_specs=(anywhere, anywhere, smem),
+        scratch_shapes=[dma((2,))],
+    )(*(pltpu.with_memory_space_constraint(x, vmem) for x in (res, tan, total)))
 
 
 def solution(mesh):

time: 22.4 us -> 19.8 us (0.88)
  local copies, waits for them, and re-layouts: 2.61 us -> 0 us
    unnamed x7 -> x0, local copies, waits for them, and re-layouts: 2.61 us -> none
    pallas_call x1 -> x2, Pallas kernels: 18.9 us -> 19 us  [the longest x1 17.8 us: local(): pl.pallas_call(functools.partial(kernel, sizes), out_shape=(vmem(shape.sh...]
where the time goes in v2:
time: 19.8 us; the launch traced here: 19.6 us
  Pallas kernels  19 us (96%)
  between operations  0.64 us (3%)
    pallas_call x1, Pallas kernels, local(): pl.pallas_call(functools.partial(kernel, sizes), out_shape=(vmem(shape.sh...  17.8 us
    pallas_call x1, Pallas kernels, local(): pl.pallas_call(functools.partial(finish, entries), out_shape=(shape, shap...  1.17 us

profile of v2, /device:TPU:0, one launch (start us, length us, event | category | flops | bytes accessed | tf_op | source)
XLA Modules:
  0.0 19.6 jit_solution(10340415423511743743)
XLA Ops:
  0.6 17.8 %shard_map.76 = (f32[3,4,8,128]{3,2,1,0:T(8,128)S(1)}, f32[3,4,8,128]{3,2,1,0:T(8,128)S(1)}, f32[2,128]{1,0:T(2,128)S(1)}) custom-call(f32[3,3]{1,0:T(4,128)} %strain_ref.1, f32[2]{0:T(128)} %material_ref.1, f32[6,4,8,128]{3,2,1,0:T(8,128)} %bitcast.1, bf16[144,256]{1,0:T(8,128)(2,1)} %constant.4.clone.fwd_hbm, bf16[16,256]{1,0:T(8,128)(2,1)} %constant.5.clone.bwd_hbm), custom_call_target="tpu_custom_call" | custom-call | tf_op jit(solution)/shard_map/pallas_call | solution.py:417
  18.4 1.2 %shard_map.77 = (f32[3,4,8,128]{3,2,1,0:T(8,128)}, f32[3,4,8,128]{3,2,1,0:T(8,128)}, f32[2]{0:T(128)}) custom-call(f32[3,4,8,128]{3,2,1,0:T(8,128)S(1)} %get-tuple-element.6.res, f32[3,4,8,128]{3,2,1,0:T(8,128)S(1)} %get-tuple-element.7.tan, f32[2,128]{1,0:T(2,128)S(1)} %get-tuple-element.8.total), custom_call_target="tpu_custom_call" | custom-call | tf_op jit(solution)/shard_map/pallas_call | solution.py:447

commit v3 on v2

--- a/solution.py
+++ b/solution.py
@@ -252,12 +252,13 @@
     used = lax.broadcasted_iota(jnp.int32, (8, 256), 0) < 3
 
     def element(e, opening):
+        tiles = []
         for c in range(6):
-            tiles = []
             for p in range(2 * e, 2 * e + 3):
                 tiles += [main[c, p], jnp.where(used, halo[c, p], 0.0)]
-            hi, lo = hi_lo(jnp.concatenate(tiles, axis=0))
-            hi, lo = (dot(part, perm[...]).astype(BF16) for part in (hi, lo))
+        parts = dot(jnp.concatenate(hi_lo(jnp.concatenate(tiles, axis=0)), axis=0), perm[...]).astype(BF16)
+        for c in range(6):
+            hi, lo = parts[48 * c:48 * c + 48], parts[288 + 48 * c:336 + 48 * c]
             data = jnp.concatenate([hi, lo, hi, jnp.zeros((112, 256), BF16)], axis=0)
             ybuf[c] = dot(fwd[...], data)
         for half in range(2):
@@ -325,8 +326,8 @@
             hi, lo = hi_lo(back[c])
             data = jnp.concatenate([hi, lo, hi, jnp.zeros((64, 256), BF16)], axis=0)
             nodal.append(dot(bwd[...], data))
-        hi, lo = hi_lo(jnp.concatenate(nodal, axis=0) * shear)
-        both = dot(hi, perm_t[...]) + dot(lo, perm_t[...])
+        both = dot(jnp.concatenate(hi_lo(jnp.concatenate(nodal, axis=0) * shear), axis=0), perm_t[...])
+        both = both[:48] + both[48:]
         for c in range(3):
             for plane in range(2):
                 result[3 * field + c, plane] = both[c * 16 + plane * 8:c * 16 + plane * 8 + 8]

time: 19.8 us -> 19.4 us (0.980)
  Pallas kernels: 19 us -> 18.6 us
    pallas_call x1, Pallas kernels: 17.8 us -> 17.4 us  [local(): pl.pallas_call(functools.partial(kernel, sizes), out_shape=(vmem(shape.sh...]
where the time goes in v3:
time: 19.4 us; the launch traced here: 19.2 us
  Pallas kernels  18.6 us (96%)
  between operations  0.64 us (3%)
    pallas_call x1, Pallas kernels, local(): pl.pallas_call(functools.partial(kernel, sizes), out_shape=(vmem(shape.sh...  17.4 us
    pallas_call x1, Pallas kernels, local(): pl.pallas_call(functools.partial(finish, entries), out_shape=(shape, shap...  1.17 us

profile of v3, /device:TPU:0, one launch (start us, length us, event | category | flops | bytes accessed | tf_op | source)
XLA Modules:
  0.0 19.2 jit_solution(1766813556162248388)
XLA Ops:
  0.6 17.4 %shard_map.76 = (f32[3,4,8,128]{3,2,1,0:T(8,128)S(1)}, f32[3,4,8,128]{3,2,1,0:T(8,128)S(1)}, f32[2,128]{1,0:T(2,128)S(1)}) custom-call(f32[3,3]{1,0:T(4,128)} %strain_ref.1, f32[2]{0:T(128)} %material_ref.1, f32[6,4,8,128]{3,2,1,0:T(8,128)} %bitcast.1, bf16[144,256]{1,0:T(8,128)(2,1)} %constant.4.clone.fwd_hbm, bf16[16,256]{1,0:T(8,128)(2,1)} %constant.5.clone.bwd_hbm), custom_call_target="tpu_custom_call" | custom-call | tf_op jit(solution)/shard_map/pallas_call | solution.py:418
  18.1 1.2 %shard_map.77 = (f32[3,4,8,128]{3,2,1,0:T(8,128)}, f32[3,4,8,128]{3,2,1,0:T(8,128)}, f32[2]{0:T(128)}) custom-call(f32[3,4,8,128]{3,2,1,0:T(8,128)S(1)} %get-tuple-element.6.res, f32[3,4,8,128]{3,2,1,0:T(8,128)S(1)} %get-tuple-element.7.tan, f32[2,128]{1,0:T(2,128)S(1)} %get-tuple-element.8.total), custom_call_target="tpu_custom_call" | custom-call | tf_op jit(solution)/shard_map/pallas_call | solution.py:448
